TPU v7x, 128 devices: a whole 4x4x4 slice. The times are simulated.
128 devices in a mesh: gx: 16 (over z, x), gy: 8 (over y, core).
Axes of the slice: x: 4, y: 4, z: 4, core: 2. Of those that a mesh axis runs over, the one named last changes fastest.
Arguments:
- density: float32 [1024, 256, 128], P('gx', 'gy'), may hold values from -6 to 6
- slowness: float32 [1024, 256, 128], P('gx', 'gy'), may hold values from -6 to 6
- pressure_obs: float32 [1024, 256, 128], P('gx', 'gy'), may hold values from -6 to 6
- time_obs: float32 [1024, 256, 128], P('gx', 'gy'), may hold values from -6 to 6
- zone_map: int32 [1024, 256, 128], P('gx', 'gy'), may hold values from 0 to 7
- zone_low: float32 [8], replicated, may hold values from -2.5 to -0.5
- zone_high: float32 [8], replicated, may hold values from 0.5 to 2.5
Outputs:
- density_out: float32 [1024, 256, 128], P('gx', 'gy')
- slowness_out: float32 [1024, 256, 128], P('gx', 'gy')
- objective: float32 [3], replicated
All inputs are finite; a program needn't handle non-finite values.
Results may differ from a plain program's by a relative error of at most 0.00013.
Values sent between devices are 32-bit elements; how exact they have to be, the bound alone decides.
A program may use at most 128 MiB of HBM per device.

v0:
```python
import math
import jax
import jax.numpy as jnp
from jax import lax
from jax.sharding import Mesh
from jax.sharding import PartitionSpec as P

ITERS = 3
GX_GY = ("gx_0", "gx_1", "gy_0", "gy_1")
GX = ("gx_0", "gx_1")
GY = ("gy_0", "gy_1")
BETA = 1.0
ETA = 0.5
EPSILON = 1e-06


def over_axes(value, axes):
    for axis in axes:
        value = lax.psum(value, axis)
    return value


def laid_out(tiles, dim):
    tiles = jnp.moveaxis(tiles, 0, dim)
    dims = tiles.shape
    return tiles.reshape(*dims[:dim], dims[dim] * dims[dim + 1], *dims[dim + 2 :])


def copy_for_each(value, axis):
    copies = jnp.broadcast_to(value, (lax.axis_size(axis), *value.shape))
    return lax.all_to_all(copies, axis, split_axis=0, concat_axis=0, tiled=True)


def collect(value, axis, dim):
    return laid_out(copy_for_each(value, axis), dim)


def with_halo(value, sides, width):
    for axis, dim in sides:
        size, length = (lax.axis_size(axis), value.shape[dim])
        up = [(i, (i + 1) % size) for i in range(size - 1)]
        down = [(j, i) for i, j in up]
        last = lax.slice_in_dim(value, length - width, length, axis=dim)
        initial = lax.slice_in_dim(value, 0, width, axis=dim)
        before = lax.ppermute(last, axis, up)
        after = lax.ppermute(initial, axis, down)
        value = jnp.concatenate([before, value, after], axis=dim)
    return value


def cross_product(first_vec, second_vec):
    return (
        first_vec[1] * second_vec[2] - first_vec[2] * second_vec[1],
        first_vec[2] * second_vec[0] - first_vec[0] * second_vec[2],
        first_vec[0] * second_vec[1] - first_vec[1] * second_vec[0],
    )


def depth_slope(inner):
    padded = jnp.pad(inner, [(0, 0)] * (inner.ndim - 1) + [(1, 1)])
    return (padded[..., 2:] - padded[..., :-2]) * 0.5


def depth_adjoint(values):
    padded = jnp.pad(values, [(0, 0)] * (values.ndim - 1) + [(1, 1)])
    return (padded[..., :-2] - padded[..., 2:]) * 0.5


def block_slopes(padded):
    along_x = (padded[:, 2:, 1:-1] - padded[:, :-2, 1:-1]) * 0.5
    along_y = (padded[:, 1:-1, 2:] - padded[:, 1:-1, :-2]) * 0.5
    along_z = depth_slope(padded[:, 1:-1, 1:-1])
    return (along_x, along_y, along_z)


def triangle(length, upward):
    first = jnp.arange(length)[:, None]
    second = jnp.arange(length)[None, :]
    if upward:
        return (first <= second).astype(jnp.float32)
    return (first >= second).astype(jnp.float32)


def depth_prefix(values, upward):
    table = triangle(values.shape[-1], upward)
    return jnp.einsum("xyj,jk->xyk", values, table, precision=lax.Precision.HIGHEST)


def rows_prefix(values, upward):
    table = triangle(values.shape[0], not upward)
    return jnp.einsum("ij,jyz->iyz", table, values, precision=lax.Precision.HIGHEST)


def global_sums(values):
    return (over_axes(values[0], GX_GY), over_axes(values[1], GX_GY), over_axes(values[2], GX_GY))


def local(density, slowness, pressure_obs, time_obs, zone_map, zone_low, zone_high):
    size_x, size_y, depth = density.shape
    parts_x = lax.axis_size(GX)
    parts_y = lax.axis_size(GY)
    total_x = size_x * parts_x
    total_y = size_y * parts_y
    cells = float(total_x * total_y * depth)
    zscale = 1.0 / math.sqrt(depth)
    xscale = 1.0 / math.sqrt(total_x)
    lower_bound = jnp.zeros(density.shape, jnp.float32)
    upper_bound = jnp.zeros(density.shape, jnp.float32)
    for zone_index in range(zone_low.shape[0]):
        hit = zone_map == zone_index
        lower_bound = jnp.where(hit, zone_low[zone_index], lower_bound)
        upper_bound = jnp.where(hit, zone_high[zone_index], upper_bound)
    my_x = lax.axis_index(GX)
    my_y = lax.axis_index(GY)
    anchor_x = my_x * size_x
    anchor_y = my_y * size_y
    shard_ids = jnp.arange(parts_x)
    own_weight = (shard_ids == my_x).astype(jnp.float32)
    later_weight = (shard_ids > my_x).astype(jnp.float32)
    earlier_table = (shard_ids[:, None] > shard_ids[None, :]).astype(jnp.float32)
    observed_totals = collect(jnp.sum(time_obs, 0)[None], GX, 0)
    observed_later = jnp.einsum(
        "k,kyz->yz", later_weight, observed_totals, precision=lax.Precision.HIGHEST
    )
    density_now = density
    slowness_now = slowness
    history = []
    for iteration in range(ITERS):
        fields = jnp.stack((density_now, slowness_now))
        padded = with_halo(fields, ((GX, 1), (GY, 2)), 2)
        along_x, along_y, along_z = block_slopes(padded)
        first_vec = (along_x[0], along_y[0], along_z[0])
        second_vec = (along_x[1], along_y[1], along_z[1])
        crossed_wide = cross_product(first_vec, second_vec)
        toward_density = cross_product(second_vec, crossed_wide)
        toward_slowness = cross_product(crossed_wide, first_vec)
        rows_x = anchor_x - 1 + jnp.arange(size_x + 2)
        rows_y = anchor_y - 1 + jnp.arange(size_y + 2)
        inside_x = (rows_x >= 0) & (rows_x < total_x)
        inside_y = (rows_y >= 0) & (rows_y < total_y)
        inside = (inside_x[:, None] & inside_y[None, :]).astype(jnp.float32)[:, :, None]
        side_x = jnp.stack((toward_density[0], toward_slowness[0])) * inside
        side_y = jnp.stack((toward_density[1], toward_slowness[1])) * inside
        back_x = (side_x[:, :-2, 1:-1] - side_x[:, 2:, 1:-1]) * 0.5
        back_y = (side_y[:, 1:-1, :-2] - side_y[:, 1:-1, 2:]) * 0.5
        depth_parts = jnp.stack((toward_density[2], toward_slowness[2]))[:, 1:-1, 1:-1]
        back_z = depth_adjoint(depth_parts)
        crossed = tuple((member[1:-1, 1:-1] for member in crossed_wide))
        cross_term = back_x + back_y + back_z
        pressure_miss = depth_prefix(density_now, True) * zscale - pressure_obs
        running = rows_prefix(slowness_now, True)
        stacked = jnp.stack((running[-1], jnp.sum(running, 0)))[None]
        gathered = collect(stacked, GX, 0)
        befores = jnp.einsum(
            "kj,jyz->kyz", earlier_table, gathered[:, 0], precision=lax.Precision.HIGHEST
        )
        before = jnp.einsum("k,kyz->yz", own_weight, befores, precision=lax.Precision.HIGHEST)
        shard_sums = gathered[:, 1] + float(size_x) * befores
        after_early = (
            jnp.einsum("k,kyz->yz", later_weight, shard_sums, precision=lax.Precision.HIGHEST)
            * xscale
            - observed_later
        )
        time_miss = (running + before[None]) * xscale - time_obs
        backward = rows_prefix(time_miss, False)
        column_back = depth_prefix(pressure_miss, False)
        grad_density = column_back * zscale + BETA * cross_term[0]
        grad_slowness = (backward + after_early[None]) * xscale + BETA * cross_term[1]
        crossed_sq = (
            jnp.sum(crossed[0] * crossed[0])
            + jnp.sum(crossed[1] * crossed[1])
            + jnp.sum(crossed[2] * crossed[2])
        )
        local_objective = (
            0.5
            * (
                jnp.sum(pressure_miss * pressure_miss)
                + jnp.sum(time_miss * time_miss)
                + BETA * crossed_sq
            )
            / cells
        )
        local_density = jnp.sum(grad_density * grad_density)
        local_slowness = jnp.sum(grad_slowness * grad_slowness)
        objective_now, norm_density, norm_slowness = global_sums(
            (local_objective, local_density, local_slowness)
        )
        history.append(objective_now)
        moved = density_now - ETA * grad_density * lax.rsqrt(norm_density / cells + EPSILON)
        density_now = jnp.minimum(jnp.maximum(moved, lower_bound), upper_bound)
        slowness_now = slowness_now - ETA * grad_slowness * lax.rsqrt(
            norm_slowness / cells + EPSILON
        )
    objective = jnp.stack(history)
    return (density_now, slowness_now, objective)


def solution(mesh):
    torus = Mesh(mesh.devices.reshape(4, 4, 4, 2), ("gx_0", "gx_1", "gy_0", "gy_1"))
    in_specs = (
        P(GX, GY, None),
        P(GX, GY, None),
        P(GX, GY, None),
        P(GX, GY, None),
        P(GX, GY, None),
        P(),
        P(),
    )
    out_specs = (P(GX, GY, None), P(GX, GY, None), P())
    return jax.shard_map(local, mesh=torus, in_specs=in_specs, out_specs=out_specs, check_vma=False)
```

profile of v0, /device:TPU:1, one launch (start us, length us, event | category | flops | bytes accessed | tf_op | source)
XLA Modules:
  0.0 324.0 jit_solution(1561969263531289439)
XLA Ops:
  1.6 3.9 %collective-permute-start = (f32[2,2,32,128]{3,2,1,0:T(8,128)S(1)}, f32[2,2,32,128]{3,2,1,0:T(8,128)S(1)}, u32[]{:S(2)}, u32[]{:S(2)}) collective-permute-start(f32[2,2,32,128]{3,2,1,0:T(8,128)S(1)} %get-tuple-element.91), channel_id=1, source_target_pairs={{0,8},{8,16},{16,24},{24,32},{32,40},{40,48},{48,56},{56,64},{64,7... | collective-permute-start | bytes 196616 | tf_op jit(solution)/shard_map/ppermute | solution.py:45
  10.1 8.5 %all-to-all-start = ((f32[16,1,2,32,128]{4,3,2,1,0:T(8,128)}), f32[16,1,2,32,128]{4,3,2,1,0:T(8,128)}, u32[]{:S(2)}, u32[]{:S(2)}) async-start(f32[16,1,2,32,128]{4,3,2,1,0:T(8,128)} %broadcast_in_dim.119), calls=%async_computation | async-start | bytes 1048576 | tf_op jit(solution)/shard_map/all_to_all | solution.py:31
  24.5 4.6 %collective-permute-start.3 = (f32[2,68,2,128]{3,2,1,0:T(2,128)S(1)}, f32[2,68,2,128]{3,2,1,0:T(2,128)S(1)}, u32[]{:S(2)}, u32[]{:S(2)}) collective-permute-start(f32[2,68,2,128]{3,2,1,0:T(2,128)S(1)} %get-tuple-element.85), channel_id=1, source_target_pairs={{0,1},{1,2},{2,3},{3,4},{4,5},{5,6},{6,7},{8,9},{9,10},{10,11},{11... | collective-permute-start | bytes 417800 | tf_op jit(solution)/shard_map/ppermute | solution.py:45
  51.5 4.1 %multiply_reduce_fusion.11 = (f32[]{:T(128)}, f32[64,32,128]{2,1,0:T(8,128)}) fusion(f32[2,64,32,128]{3,2,1,0:T(8,128)} %fusion.23, f32[64,32,128]{2,0,1:T(8,128)S(1)} %copy-done.24), kind=kOutput, calls=%fused_computation.196 | convolution fusion | flops 403718144 | bytes 3145732 | tf_op jit(solution)/shard_map/xyj,jk->xyk/dot_general | solution.py:86
  57.8 3.9 %multiply_reduce_fusion.4 = (f32[]{:T(128)}, f32[64,32,128]{2,1,0:T(8,128)}, f32[32,128]{1,0:T(8,128)S(1)}) fusion(f32[64,32,128]{2,1,0:T(8,128)} %param.10, f32[32,128]{1,0:T(8,128)S(1)} %bitcast.239, f32[64,32,128]{2,0,1:T(8,128)} %copy-done.19), kind=kLoop, calls=%fused_computation.181 | loop fusion | flops 1568767 | bytes 3178500 | tf_op jit(solution)/shard_map/reduce_sum | solution.py:178
  62.5 7.2 %all-to-all-start.1 = ((f32[16,1,32,128]{3,2,1,0:T(8,128)}), f32[16,1,32,128]{3,2,1,0:T(8,128)}, u32[]{:S(2)}, u32[]{:S(2)}) async-start(f32[16,1,32,128]{3,2,1,0:T(8,128)} %broadcast_in_dim.120), calls=%async_computation.1 | async-start | bytes 524288 | tf_op jit(solution)/shard_map/all_to_all | solution.py:31
  81.0 7.5 %all-reduce.14 = (f32[]{:T(128)}, f32[]{:T(128)}) all-reduce(f32[]{:T(128)} %get-tuple-element.124, f32[]{:T(128)} %multiply_reduce_fusion.10), channel_id=1, replica_groups=mesh['gx_0'=4,'gx_1'=4,'gy_0'=4,'gy_1'=2] {'gx_0'}, use_global_device_ids=true, to_apply=%region_1.2 | all-reduce | flops 2 | bytes 16 | tf_op jit(solution)/shard_map/psum | solution.py:19
  88.6 9.2 %all-reduce.11 = (f32[]{:T(128)}, f32[]{:T(128)}) all-reduce(f32[]{:T(128)} %get-tuple-element.28, f32[]{:T(128)} %get-tuple-element.29), channel_id=1, replica_groups=mesh['gx_0'=4,'gx_1'=4,'gy_0'=4,'gy_1'=2] {'gx_1'}, use_global_device_ids=true, to_apply=%region_2.3 | all-reduce | flops 2 | bytes 16 | tf_op jit(solution)/shard_map/psum | solution.py:19
  97.8 7.7 %all-reduce.8 = (f32[]{:T(128)}, f32[]{:T(128)}) all-reduce(f32[]{:T(128)} %get-tuple-element.19, f32[]{:T(128)} %get-tuple-element.20), channel_id=1, replica_groups=mesh['gx_0'=4,'gx_1'=4,'gy_0'=4,'gy_1'=2] {'gy_0'}, use_global_device_ids=true, to_apply=%region_3.4 | all-reduce | flops 2 | bytes 16 | tf_op jit(solution)/shard_map/psum | solution.py:19
  105.6 9.5 %all-reduce.17 = (f32[]{:T(128)}, f32[]{:T(128)}) all-reduce(f32[]{:T(128)} %get-tuple-element.10, f32[]{:T(128)} %get-tuple-element.11), channel_id=1, replica_groups=mesh['gx_0'=4,'gx_1'=4,'gy_0'=4,'gy_1'=2] {'gy_1'}, use_global_device_ids=true, to_apply=%region_4.5 | all-reduce | flops 2 | bytes 16 | tf_op jit(solution)/shard_map/psum | solution.py:19
  118.7 14.6 %maximum_minimum_fusion.2 = (f32[64,32,128]{2,1,0:T(8,128)S(1)}, f32[64,32,128]{2,1,0:T(8,128)}, f32[64,32,128]{2,1,0:T(8,128)}) fusion(f32[64,32,128]{2,1,0:T(8,128)} %param.7, f32[64,32,128]{2,1,0:T(8,128)} %get-tuple-element.125, f32[]{:T(128)S(6)} %mul.590, pred[64,32,128]{2,1,0:T(8,128)(4,1)} %get-tuple-element.99, ...), kind=kLoop, calls=%fused_computation.194 | loop fusion | flops 5242880 | bytes 7340100 | tf_op jit(solution)/shard_map/min | solution.py:190
  140.0 3.9 %collective-permute-start.7 = (f32[2,68,2,128]{3,2,1,0:T(2,128)S(1)}, f32[2,68,2,128]{3,2,1,0:T(2,128)S(1)}, u32[]{:S(2)}, u32[]{:S(2)}) collective-permute-start(f32[2,68,2,128]{3,2,1,0:T(2,128)S(1)} %get-tuple-element.83), channel_id=1, source_target_pairs={{0,1},{1,2},{2,3},{3,4},{4,5},{5,6},{6,7},{8,9},{9,10},{10,11},{11... | collective-permute-start | bytes 417800 | tf_op jit(solution)/shard_map/ppermute | solution.py:45
  149.1 7.0 %all-to-all-start.2 = ((f32[16,1,2,32,128]{4,3,2,1,0:T(8,128)}), f32[16,1,2,32,128]{4,3,2,1,0:T(8,128)}, u32[]{:S(2)}, u32[]{:S(2)}) async-start(f32[16,1,2,32,128]{4,3,2,1,0:T(8,128)} %broadcast_in_dim.121), calls=%async_computation.2 | async-start | bytes 1048576 | tf_op jit(solution)/shard_map/all_to_all | solution.py:31
  174.0 3.9 %multiply_reduce_fusion.9 = (f32[]{:T(128)}, f32[64,32,128]{2,1,0:T(8,128)}) fusion(f32[2,64,32,128]{3,2,1,0:T(8,128)} %fusion.20, f32[64,32,128]{2,1,0:T(8,128)} %get-tuple-element.139), kind=kOutput, calls=%fused_computation.190 | convolution fusion | flops 403718144 | bytes 3145732 | tf_op jit(solution)/shard_map/xyj,jk->xyk/dot_general | solution.py:86
  184.0 9.4 %all-reduce.13 = (f32[]{:T(128)}, f32[]{:T(128)}) all-reduce(f32[]{:T(128)} %get-tuple-element.128, f32[]{:T(128)} %multiply_reduce_fusion.8), channel_id=1, replica_groups=mesh['gx_0'=4,'gx_1'=4,'gy_0'=4,'gy_1'=2] {'gx_0'}, use_global_device_ids=true, to_apply=%region_13.14 | all-reduce | flops 2 | bytes 16 | tf_op jit(solution)/shard_map/psum | solution.py:19
  193.3 9.0 %all-reduce.10 = (f32[]{:T(128)}, f32[]{:T(128)}) all-reduce(f32[]{:T(128)} %get-tuple-element.26, f32[]{:T(128)} %get-tuple-element.27), channel_id=1, replica_groups=mesh['gx_0'=4,'gx_1'=4,'gy_0'=4,'gy_1'=2] {'gx_1'}, use_global_device_ids=true, to_apply=%region_14.15 | all-reduce | flops 2 | bytes 16 | tf_op jit(solution)/shard_map/psum | solution.py:19
  202.3 7.1 %all-reduce.7 = (f32[]{:T(128)}, f32[]{:T(128)}) all-reduce(f32[]{:T(128)} %get-tuple-element.17, f32[]{:T(128)} %get-tuple-element.18), channel_id=1, replica_groups=mesh['gx_0'=4,'gx_1'=4,'gy_0'=4,'gy_1'=2] {'gy_0'}, use_global_device_ids=true, to_apply=%region_15.16 | all-reduce | flops 2 | bytes 16 | tf_op jit(solution)/shard_map/psum | solution.py:19
  209.4 10.8 %all-reduce.16 = (f32[]{:T(128)}, f32[]{:T(128)}) all-reduce(f32[]{:T(128)} %get-tuple-element.8, f32[]{:T(128)} %get-tuple-element.9), channel_id=1, replica_groups=mesh['gx_0'=4,'gx_1'=4,'gy_0'=4,'gy_1'=2] {'gy_1'}, use_global_device_ids=true, to_apply=%region_16.17 | all-reduce | flops 2 | bytes 16 | tf_op jit(solution)/shard_map/psum | solution.py:19
  241.7 7.1 %all-to-all-start.3 = ((f32[16,1,2,32,128]{4,3,2,1,0:T(8,128)}), f32[16,1,2,32,128]{4,3,2,1,0:T(8,128)}, u32[]{:S(2)}, u32[]{:S(2)}) async-start(f32[16,1,2,32,128]{4,3,2,1,0:T(8,128)} %broadcast_in_dim.122), calls=%async_computation.3 | async-start | bytes 1048576 | tf_op jit(solution)/shard_map/all_to_all | solution.py:31
  266.6 3.8 %multiply_reduce_fusion.7 = (f32[]{:T(128)}, f32[64,32,128]{2,1,0:T(8,128)}) fusion(f32[2,64,32,128]{3,2,1,0:T(8,128)} %fusion.17, f32[64,32,128]{2,1,0:T(8,128)} %get-tuple-element.137), kind=kOutput, calls=%fused_computation.186 | convolution fusion | flops 403718144 | bytes 3145732 | tf_op jit(solution)/shard_map/xyj,jk->xyk/dot_general | solution.py:86
  279.0 9.4 %all-reduce.12 = (f32[]{:T(128)}, f32[]{:T(128)}, f32[]{:T(128)}, f32[]{:T(128)}, f32[]{:T(128)}) all-reduce(f32[]{:T(128)} %get-tuple-element.132, f32[]{:T(128)} %multiply_reduce_fusion.6, f32[]{:T(128)S(6)} %div.35, f32[]{:T(128)S(6)} %div.34, f32[]{:T(128)S(6)} %div.33), channel_id=1, replica_groups=mesh['gx_0'=4,'gx_1'=4,'gy_0'=4,'gy_1'=2] {'gx_0'}, use_global_device_ids=true, to_apply=%region_24.25 | all-reduce | flops 5 | bytes 40 | tf_op jit(solution)/shard_map/psum | solution.py:19
  288.4 9.1 %all-reduce.9 = (f32[]{:T(128)}, f32[]{:T(128)}, f32[]{:T(128)}, f32[]{:T(128)}, f32[]{:T(128)}) all-reduce(f32[]{:T(128)} %get-tuple-element.21, f32[]{:T(128)} %get-tuple-element.22, f32[]{:T(128)} %get-tuple-element.23, f32[]{:T(128)} %get-tuple-element.24, ...), channel_id=1, replica_groups=mesh['gx_0'=4,'gx_1'=4,'gy_0'=4,'gy_1'=2] {'gx_1'}, use_global_device_ids=true, to_apply=%region_25.26 | all-reduce | flops 5 | bytes 40 | tf_op jit(solution)/shard_map/psum | solution.py:19
  297.4 7.4 %all-reduce.6 = (f32[]{:T(128)}, f32[]{:T(128)}, f32[]{:T(128)}, f32[]{:T(128)}, f32[]{:T(128)}) all-reduce(f32[]{:T(128)} %get-tuple-element.12, f32[]{:T(128)} %get-tuple-element.13, f32[]{:T(128)} %get-tuple-element.14, f32[]{:T(128)} %get-tuple-element.15, ...), channel_id=1, replica_groups=mesh['gx_0'=4,'gx_1'=4,'gy_0'=4,'gy_1'=2] {'gy_0'}, use_global_device_ids=true, to_apply=%region_26.27 | all-reduce | flops 5 | bytes 40 | tf_op jit(solution)/shard_map/psum | solution.py:19
  304.9 10.5 %all-reduce.15 = (f32[]{:T(128)}, f32[]{:T(128)}, f32[1]{0:T(128)}, f32[1]{0:T(128)}, f32[1]{0:T(128)}) all-reduce(f32[]{:T(128)} %get-tuple-element.3, f32[]{:T(128)} %get-tuple-element.4, f32[1]{0:T(128)} %bitcast.79, f32[1]{0:T(128)} %bitcast.75, f32[1]{0:T(128)} %bitcast.71), channel_id=1, replica_groups=mesh['gx_0'=4,'gx_1'=4,'gy_0'=4,'gy_1'=2] {'gy_1'}, use_global_device_ids=true, to_apply=%region_27.28 | all-reduce | flops 5 | bytes 40 | tf_op jit(solution)/shard_map/psum | solution.py:19
  (184 shorter events, 130.1 us)
Async XLA Ops:
  0.6 6.3 %copy-start = (f32[64,32,128]{2,1,0:T(8,128)S(1)}, f32[64,32,128]{2,1,0:T(8,128)}, u32[]{:S(2)}) copy-start(f32[64,32,128]{2,1,0:T(8,128)} %param.8) | copy-start | bytes 3145732
  0.6 18.1 %copy-start.1 = (f32[64,32,128]{2,1,0:T(8,128)S(1)}, f32[64,32,128]{2,1,0:T(8,128)}, u32[]{:S(2)}) copy-start(f32[64,32,128]{2,1,0:T(8,128)} %param.7) | copy-start | bytes 3145732
  0.7 18.1 %copy-start.6 = (f32[64,32,128]{2,1,0:T(8,128)S(1)}, f32[64,32,128]{2,1,0:T(8,128)}, u32[]{:S(2)}) copy-start(f32[64,32,128]{2,1,0:T(8,128)} %param.9) | copy-start | bytes 3145732
  1.6 22.7 %collective-permute-start = (f32[2,2,32,128]{3,2,1,0:T(8,128)S(1)}, f32[2,2,32,128]{3,2,1,0:T(8,128)S(1)}, u32[]{:S(2)}, u32[]{:S(2)}) collective-permute-start(f32[2,2,32,128]{3,2,1,0:T(8,128)S(1)} %get-tuple-element.91), channel_id=1, source_target_pairs={{0,8},{8,16},{16,24},{24,32},{32,40},{40,48},{48,56},{56,64},{64,7... | collective-permute-start | bytes 196616 | tf_op jit(solution)/shard_map/ppermute | solution.py:45
  5.6 18.8 %collective-permute-start.1 = (f32[2,2,32,128]{3,2,1,0:T(8,128)S(1)}, f32[2,2,32,128]{3,2,1,0:T(8,128)S(1)}, u32[]{:S(2)}, u32[]{:S(2)}) collective-permute-start(f32[2,2,32,128]{3,2,1,0:T(8,128)S(1)} %get-tuple-element.92), channel_id=1, source_target_pairs={{8,0},{16,8},{24,16},{32,24},{40,32},{48,40},{56,48},{64,56},{72,6... | collective-permute-start | bytes 196616 | tf_op jit(solution)/shard_map/ppermute | solution.py:46
  10.1 45.5 %all-to-all-start = ((f32[16,1,2,32,128]{4,3,2,1,0:T(8,128)}), f32[16,1,2,32,128]{4,3,2,1,0:T(8,128)}, u32[]{:S(2)}, u32[]{:S(2)}) async-start(f32[16,1,2,32,128]{4,3,2,1,0:T(8,128)} %broadcast_in_dim.119), calls=%async_computation | async-start | bytes 1048576 | tf_op jit(solution)/shard_map/all_to_all | solution.py:31
  22.1 9.1 %copy-start.29 = (f32[8]{0:T(128)S(1)}, f32[8]{0:T(128)}, u32[]{:S(2)}) copy-start(f32[8]{0:T(128)} %param.12) | copy-start | bytes 100
  22.1 9.8 %copy-start.30 = (f32[8]{0:T(128)S(1)}, f32[8]{0:T(128)}, u32[]{:S(2)}) copy-start(f32[8]{0:T(128)} %param.13) | copy-start | bytes 100
  24.5 8.1 %collective-permute-start.3 = (f32[2,68,2,128]{3,2,1,0:T(2,128)S(1)}, f32[2,68,2,128]{3,2,1,0:T(2,128)S(1)}, u32[]{:S(2)}, u32[]{:S(2)}) collective-permute-start(f32[2,68,2,128]{3,2,1,0:T(2,128)S(1)} %get-tuple-element.85), channel_id=1, source_target_pairs={{0,1},{1,2},{2,3},{3,4},{4,5},{5,6},{6,7},{8,9},{9,10},{10,11},{11... | collective-permute-start | bytes 417800 | tf_op jit(solution)/shard_map/ppermute | solution.py:45
  29.1 6.4 %collective-permute-start.2 = (f32[2,68,2,128]{3,2,1,0:T(2,128)S(1)}, f32[2,68,2,128]{3,2,1,0:T(2,128)S(1)}, u32[]{:S(2)}, u32[]{:S(2)}) collective-permute-start(f32[2,68,2,128]{3,2,1,0:T(2,128)S(1)} %get-tuple-element.86), channel_id=1, source_target_pairs={{1,0},{2,1},{3,2},{4,3},{5,4},{6,5},{7,6},{9,8},{10,9},{11,10},{12... | collective-permute-start | bytes 417800 | tf_op jit(solution)/shard_map/ppermute | solution.py:46
  57.8 20.7 %copy-start.3 = (f32[2,64,32,128]{3,2,1,0:T(8,128)S(1)}, f32[2,64,32,128]{3,2,1,0:T(8,128)}, u32[]{:S(2)}) copy-start(f32[2,64,32,128]{3,2,1,0:T(8,128)} %fusion.23) | copy-start | bytes 6291460
  62.5 14.7 %all-to-all-start.1 = ((f32[16,1,32,128]{3,2,1,0:T(8,128)}), f32[16,1,32,128]{3,2,1,0:T(8,128)}, u32[]{:S(2)}, u32[]{:S(2)}) async-start(f32[16,1,32,128]{3,2,1,0:T(8,128)} %broadcast_in_dim.120), calls=%async_computation.1 | async-start | bytes 524288 | tf_op jit(solution)/shard_map/all_to_all | solution.py:31
  78.5 40.1 %copy-start.28 = (pred[64,32,128]{2,1,0:T(8,128)(4,1)S(1)}, pred[64,32,128]{2,1,0:T(8,128)(4,1)}, u32[]{:S(2)}) copy-start(pred[64,32,128]{2,1,0:T(8,128)(4,1)} %get-tuple-element.93) | copy-start | bytes 786436
  133.3 5.1 %collective-permute-start.4 = (f32[2,2,32,128]{3,2,1,0:T(8,128)S(1)}, f32[2,2,32,128]{3,2,1,0:T(8,128)S(1)}, u32[]{:S(2)}, u32[]{:S(2)}) collective-permute-start(f32[2,2,32,128]{3,2,1,0:T(8,128)S(1)} %get-tuple-element.89), channel_id=1, source_target_pairs={{0,8},{8,16},{16,24},{24,32},{32,40},{40,48},{48,56},{56,64},{64,7... | collective-permute-start | bytes 196616 | tf_op jit(solution)/shard_map/ppermute | solution.py:45
  134.9 5.0 %collective-permute-start.5 = (f32[2,2,32,128]{3,2,1,0:T(8,128)S(1)}, f32[2,2,32,128]{3,2,1,0:T(8,128)S(1)}, u32[]{:S(2)}, u32[]{:S(2)}) collective-permute-start(f32[2,2,32,128]{3,2,1,0:T(8,128)S(1)} %get-tuple-element.90), channel_id=1, source_target_pairs={{8,0},{16,8},{24,16},{32,24},{40,32},{48,40},{56,48},{64,56},{72,6... | collective-permute-start | bytes 196616 | tf_op jit(solution)/shard_map/ppermute | solution.py:46
  140.0 16.1 %collective-permute-start.7 = (f32[2,68,2,128]{3,2,1,0:T(2,128)S(1)}, f32[2,68,2,128]{3,2,1,0:T(2,128)S(1)}, u32[]{:S(2)}, u32[]{:S(2)}) collective-permute-start(f32[2,68,2,128]{3,2,1,0:T(2,128)S(1)} %get-tuple-element.83), channel_id=1, source_target_pairs={{0,1},{1,2},{2,3},{3,4},{4,5},{5,6},{6,7},{8,9},{9,10},{10,11},{11... | collective-permute-start | bytes 417800 | tf_op jit(solution)/shard_map/ppermute | solution.py:45
  143.9 12.2 %collective-permute-start.6 = (f32[2,68,2,128]{3,2,1,0:T(2,128)S(1)}, f32[2,68,2,128]{3,2,1,0:T(2,128)S(1)}, u32[]{:S(2)}, u32[]{:S(2)}) collective-permute-start(f32[2,68,2,128]{3,2,1,0:T(2,128)S(1)} %get-tuple-element.84), channel_id=1, source_target_pairs={{1,0},{2,1},{3,2},{4,3},{5,4},{6,5},{7,6},{9,8},{10,9},{11,10},{12... | collective-permute-start | bytes 417800 | tf_op jit(solution)/shard_map/ppermute | solution.py:46
  149.1 28.7 %all-to-all-start.2 = ((f32[16,1,2,32,128]{4,3,2,1,0:T(8,128)}), f32[16,1,2,32,128]{4,3,2,1,0:T(8,128)}, u32[]{:S(2)}, u32[]{:S(2)}) async-start(f32[16,1,2,32,128]{4,3,2,1,0:T(8,128)} %broadcast_in_dim.121), calls=%async_computation.2 | async-start | bytes 1048576 | tf_op jit(solution)/shard_map/all_to_all | solution.py:31
  226.1 4.8 %collective-permute-start.8 = (f32[2,2,32,128]{3,2,1,0:T(8,128)S(1)}, f32[2,2,32,128]{3,2,1,0:T(8,128)S(1)}, u32[]{:S(2)}, u32[]{:S(2)}) collective-permute-start(f32[2,2,32,128]{3,2,1,0:T(8,128)S(1)} %get-tuple-element.87), channel_id=1, source_target_pairs={{0,8},{8,16},{16,24},{24,32},{32,40},{40,48},{48,56},{56,64},{64,7... | collective-permute-start | bytes 196616 | tf_op jit(solution)/shard_map/ppermute | solution.py:45
  227.4 5.0 %collective-permute-start.9 = (f32[2,2,32,128]{3,2,1,0:T(8,128)S(1)}, f32[2,2,32,128]{3,2,1,0:T(8,128)S(1)}, u32[]{:S(2)}, u32[]{:S(2)}) collective-permute-start(f32[2,2,32,128]{3,2,1,0:T(8,128)S(1)} %get-tuple-element.88), channel_id=1, source_target_pairs={{8,0},{16,8},{24,16},{32,24},{40,32},{48,40},{56,48},{64,56},{72,6... | collective-permute-start | bytes 196616 | tf_op jit(solution)/shard_map/ppermute | solution.py:46
  233.2 15.6 %collective-permute-start.11 = (f32[2,68,2,128]{3,2,1,0:T(2,128)}, f32[2,68,2,128]{3,2,1,0:T(2,128)S(1)}, u32[]{:S(2)}, u32[]{:S(2)}) collective-permute-start(f32[2,68,2,128]{3,2,1,0:T(2,128)} %get-tuple-element.81), channel_id=1, source_target_pairs={{0,1},{1,2},{2,3},{3,4},{4,5},{5,6},{6,7},{8,9},{9,10},{10,11},{11... | collective-permute-start | bytes 417800 | tf_op jit(solution)/shard_map/ppermute | solution.py:45
  236.2 12.6 %collective-permute-start.10 = (f32[2,68,2,128]{3,2,1,0:T(2,128)}, f32[2,68,2,128]{3,2,1,0:T(2,128)}, u32[]{:S(2)}, u32[]{:S(2)}) collective-permute-start(f32[2,68,2,128]{3,2,1,0:T(2,128)} %get-tuple-element.82), channel_id=1, source_target_pairs={{1,0},{2,1},{3,2},{4,3},{5,4},{6,5},{7,6},{9,8},{10,9},{11,10},{12... | collective-permute-start | bytes 417800 | tf_op jit(solution)/shard_map/ppermute | solution.py:46
  239.5 10.6 %copy-start.20 = (f32[64,32,128]{2,0,1:T(8,128)}, f32[64,32,128]{2,0,1:T(8,128)S(1)}, u32[]{:S(2)}) copy-start(f32[64,32,128]{2,0,1:T(8,128)S(1)} %get-tuple-element.135) | copy-start | bytes 3145732
  241.7 28.8 %all-to-all-start.3 = ((f32[16,1,2,32,128]{4,3,2,1,0:T(8,128)}), f32[16,1,2,32,128]{4,3,2,1,0:T(8,128)}, u32[]{:S(2)}, u32[]{:S(2)}) async-start(f32[16,1,2,32,128]{4,3,2,1,0:T(8,128)} %broadcast_in_dim.122), calls=%async_computation.3 | async-start | bytes 1048576 | tf_op jit(solution)/shard_map/all_to_all | solution.py:31
  (23 other events, 57.8 us)
where the time goes:
time: 330 us; the launch traced here: 324 us
  blocking collectives  107 us (32%)
  other arithmetic  89.5 us (27%)
  starting transfers between devices  58 us (18%)
  matrix products  33.9 us (10%)
  between operations  14.7 us (4%)
  local copies, waits for them, and re-layouts  13.6 us (4%)
  waiting for transfers between devices  7.63 us (2%)
    psum x12, blocking collectives, over_axes(): value = lax.psum(value, axis)  107 us
    all_to_all x4, starting transfers between devices, copy_for_each(): return lax.all_to_all(copies, axis, split_axis=0, concat_axis=0, tiled=True)  29.8 us
    dot_general x6, matrix products, depth_prefix(): jnp.einsum('xyj,jk->xyk', values, table, precision=lax.Precision.HIGHEST)  19.6 us
    min x3, other arithmetic, local(): density_now = jnp.minimum(jnp.maximum(moved, lower_bound), upper_bound)  18.5 us
    ppermute x6, starting transfers between devices, with_halo(): before = lax.ppermute(last, axis, up)  18.4 us
    dot_general x6, matrix products, rows_prefix(): jnp.einsum('ij,jyz->iyz', table, values, precision=lax.Precision.HIGHEST)  9.99 us
    ppermute x6, starting transfers between devices, with_halo(): after = lax.ppermute(initial, axis, down)  9.84 us
    sub x3, other arithmetic, local(): slowness_now - ETA * grad_slowness * lax.rsqrt(norm_slowness / cells + EP...  7.55 us
  transfers between devices with their start and end apart: 16, of which 4 were waited for; matrix products, arithmetic and copies ran while one was open for 24% of the time, Pallas kernels for 0%

commit v1 on v0

--- a/solution.py
+++ b/solution.py
@@ -12,11 +12,12 @@
 BETA = 1.0
 ETA = 0.5
 EPSILON = 1e-06
+produce_joints = lambda load, axis_name: lax.all_gather(load, axis_name=axis_name).sum(axis=0)
 
 
 def over_axes(value, axes):
     for axis in axes:
-        value = lax.psum(value, axis)
+        value = produce_joints(value, axis)
     return value
 
 

time: 330 us -> 396 us (1.20)
  local copies, waits for them, and re-layouts: 13.6 us -> 64.7 us
  other arithmetic: 89.5 us -> 113 us
  blocking collectives: 107 us -> 98.7 us
    psum x12 -> x0, blocking collectives: 107 us -> none  [over_axes(): value = lax.psum(value, axis)]
    unnamed x0 -> x12, blocking collectives: none -> 98.7 us
    unnamed x62 -> x146, local copies, waits for them, and re-layouts: 4.66 us -> 55.7 us
    reduce_sum x0 -> x36, other arithmetic: none -> 22.2 us  [lax.all_gather(load, axis_name=axis_name).sum(axis=0)]
  transfers between devices with their start and end apart: 16 -> 16, of which waited for: 4 -> 4; matrix products, arithmetic and copies ran while one was open for 24% -> 20% of each run, Pallas kernels for 0% -> 0%
where the time goes in v1:
time: 396 us; the launch traced here: 389 us
  other arithmetic  113 us (29%)
  blocking collectives  98.7 us (25%)
  local copies, waits for them, and re-layouts  64.7 us (16%)
  starting transfers between devices  59 us (15%)
  matrix products  32.2 us (8%)
  between operations  15.6 us (4%)
  waiting for transfers between devices  6.3 us (2%)
    unnamed x12, blocking collectives  98.7 us
    unnamed x146, local copies, waits for them, and re-layouts  55.7 us
    all_to_all x4, starting transfers between devices, copy_for_each(): return lax.all_to_all(copies, axis, split_axis=0, concat_axis=0, tiled=True)  29.7 us
    reduce_sum x36, other arithmetic, lax.all_gather(load, axis_name=axis_name).sum(axis=0)  22.2 us
    min x3, other arithmetic, local(): density_now = jnp.minimum(jnp.maximum(moved, lower_bound), upper_bound)  20.4 us
    ppermute x6, starting transfers between devices, with_halo(): before = lax.ppermute(last, axis, up)  19.3 us
    dot_general x6, matrix products, depth_prefix(): jnp.einsum('xyj,jk->xyk', values, table, precision=lax.Precision.HIGHEST)  17.9 us
    dot_general x6, matrix products, rows_prefix(): jnp.einsum('ij,jyz->iyz', table, values, precision=lax.Precision.HIGHEST)  9.98 us
  transfers between devices with their start and end apart: 16, of which 4 were waited for; matrix products, arithmetic and copies ran while one was open for 20% of the time, Pallas kernels for 0%

profile of v1, /device:TPU:1, one launch (start us, length us, event | category | flops | bytes accessed | tf_op | source)
XLA Modules:
  0.0 389.5 jit_solution(5007123911853393426)
XLA Ops:
  1.6 3.9 %collective-permute-start = (f32[2,2,32,128]{3,2,1,0:T(8,128)S(1)}, f32[2,2,32,128]{3,2,1,0:T(8,128)S(1)}, u32[]{:S(2)}, u32[]{:S(2)}) collective-permute-start(f32[2,2,32,128]{3,2,1,0:T(8,128)S(1)} %get-tuple-element.91), channel_id=1, source_target_pairs={{0,8},{8,16},{16,24},{24,32},{32,40},{40,48},{48,56},{56,64},{64,7... | collective-permute-start | bytes 196616 | tf_op jit(solution)/shard_map/ppermute | solution.py:46
  10.1 8.5 %all-to-all-start = ((f32[16,1,2,32,128]{4,3,2,1,0:T(8,128)}), f32[16,1,2,32,128]{4,3,2,1,0:T(8,128)}, u32[]{:S(2)}, u32[]{:S(2)}) async-start(f32[16,1,2,32,128]{4,3,2,1,0:T(8,128)} %broadcast_in_dim.119), calls=%async_computation | async-start | bytes 1048576 | tf_op jit(solution)/shard_map/all_to_all | solution.py:32
  24.5 4.6 %collective-permute-start.3 = (f32[2,68,2,128]{3,2,1,0:T(2,128)S(1)}, f32[2,68,2,128]{3,2,1,0:T(2,128)S(1)}, u32[]{:S(2)}, u32[]{:S(2)}) collective-permute-start(f32[2,68,2,128]{3,2,1,0:T(2,128)S(1)} %get-tuple-element.85), channel_id=1, source_target_pairs={{0,1},{1,2},{2,3},{3,4},{4,5},{5,6},{6,7},{8,9},{9,10},{10,11},{11... | collective-permute-start | bytes 417800 | tf_op jit(solution)/shard_map/ppermute | solution.py:46
  51.5 4.0 %multiply_reduce_fusion.11 = (f32[]{:T(128)}, f32[64,32,128]{2,1,0:T(8,128)}) fusion(f32[2,64,32,128]{3,2,1,0:T(8,128)} %fusion.23, f32[64,32,128]{2,0,1:T(8,128)S(1)} %copy-done.24), kind=kOutput, calls=%fused_computation.196 | convolution fusion | flops 403718144 | bytes 3145732 | tf_op jit(solution)/shard_map/xyj,jk->xyk/dot_general | solution.py:87
  59.0 4.0 %multiply_reduce_fusion.4 = (f32[]{:T(128)}, f32[64,32,128]{2,1,0:T(8,128)}, f32[32,128]{1,0:T(8,128)S(1)}) fusion(f32[64,32,128]{2,1,0:T(8,128)} %param.10, f32[32,128]{1,0:T(8,128)S(1)} %bitcast.279, f32[64,32,128]{2,0,1:T(8,128)} %copy-done.19), kind=kLoop, calls=%fused_computation.181 | loop fusion | flops 1568767 | bytes 3178500 | tf_op jit(solution)/shard_map/reduce_sum | solution.py:179
  63.7 7.3 %all-to-all-start.1 = ((f32[16,1,32,128]{3,2,1,0:T(8,128)}), f32[16,1,32,128]{3,2,1,0:T(8,128)}, u32[]{:S(2)}, u32[]{:S(2)}) async-start(f32[16,1,32,128]{3,2,1,0:T(8,128)} %broadcast_in_dim.120), calls=%async_computation.1 | async-start | bytes 524288 | tf_op jit(solution)/shard_map/all_to_all | solution.py:32
  71.1 3.4 fusion.59
  85.2 6.6 %all-reduce.50 = (f32[4]{0:T(128)S(1)}, f32[4]{0:T(128)S(1)}) all-reduce(f32[4]{0:T(128)S(1)} %dynamic-update-slice, f32[4]{0:T(128)S(1)} %dynamic-update-slice.4), channel_id=1, replica_groups=mesh['gx_0'=4,'gx_1'=4,'gy_0'=4,'gy_1'=2] {'gx_0'}, use_global_device_ids=true, to_apply=%add.6 | all-reduce | flops 8 | bytes 64
  96.0 7.5 %all-reduce.47 = (f32[4]{0:T(128)S(1)}, f32[4]{0:T(128)S(1)}) all-reduce(f32[4]{0:T(128)S(1)} %dynamic-update-slice.1, f32[4]{0:T(128)S(1)} %dynamic-update-slice.5), channel_id=1, replica_groups=mesh['gx_0'=4,'gx_1'=4,'gy_0'=4,'gy_1'=2] {'gx_1'}, use_global_device_ids=true, to_apply=%add.7 | all-reduce | flops 8 | bytes 64
  107.5 7.5 %all-reduce.44 = (f32[4]{0:T(128)S(1)}, f32[4]{0:T(128)S(1)}) all-reduce(f32[4]{0:T(128)S(1)} %dynamic-update-slice.2, f32[4]{0:T(128)S(1)} %dynamic-update-slice.6), channel_id=1, replica_groups=mesh['gx_0'=4,'gx_1'=4,'gy_0'=4,'gy_1'=2] {'gy_0'}, use_global_device_ids=true, to_apply=%add.8 | all-reduce | flops 8 | bytes 64
  119.6 10.2 %all-reduce.53 = (f32[2]{0:T(128)S(1)}, f32[2]{0:T(128)S(1)}) all-reduce(f32[2]{0:T(128)S(1)} %dynamic-update-slice.3, f32[2]{0:T(128)S(1)} %dynamic-update-slice.7), channel_id=1, replica_groups=mesh['gx_0'=4,'gx_1'=4,'gy_0'=4,'gy_1'=2] {'gy_1'}, use_global_device_ids=true, to_apply=%add.9 | all-reduce | flops 4 | bytes 32
  134.6 14.7 %maximum_minimum_fusion.2 = (f32[64,32,128]{2,1,0:T(8,128)S(1)}, f32[64,32,128]{2,1,0:T(8,128)}, f32[64,32,128]{2,1,0:T(8,128)}) fusion(f32[64,32,128]{2,1,0:T(8,128)} %param.7, f32[64,32,128]{2,1,0:T(8,128)} %get-tuple-element.125, f32[]{:T(128)S(6)} %mul.590, pred[64,32,128]{2,1,0:T(8,128)(4,1)} %get-tuple-element.99, ...), kind=kLoop, calls=%fused_computation.194 | loop fusion | flops 5242880 | bytes 7340100 | tf_op jit(solution)/shard_map/min | solution.py:191
  165.5 6.9 %all-to-all-start.2 = ((f32[16,1,2,32,128]{4,3,2,1,0:T(8,128)}), f32[16,1,2,32,128]{4,3,2,1,0:T(8,128)}, u32[]{:S(2)}, u32[]{:S(2)}) async-start(f32[16,1,2,32,128]{4,3,2,1,0:T(8,128)} %broadcast_in_dim.121), calls=%async_computation.2 | async-start | bytes 1048576 | tf_op jit(solution)/shard_map/all_to_all | solution.py:32
  197.4 8.6 %all-reduce.49 = (f32[4]{0:T(128)S(1)}, f32[4]{0:T(128)S(1)}) all-reduce(f32[4]{0:T(128)S(1)} %dynamic-update-slice.8, f32[4]{0:T(128)S(1)} %dynamic-update-slice.12), channel_id=1, replica_groups=mesh['gx_0'=4,'gx_1'=4,'gy_0'=4,'gy_1'=2] {'gx_0'}, use_global_device_ids=true, to_apply=%add.14 | all-reduce | flops 8 | bytes 64
  212.4 8.4 %all-reduce.46 = (f32[4]{0:T(128)S(1)}, f32[4]{0:T(128)S(1)}) all-reduce(f32[4]{0:T(128)S(1)} %dynamic-update-slice.9, f32[4]{0:T(128)S(1)} %dynamic-update-slice.13), channel_id=1, replica_groups=mesh['gx_0'=4,'gx_1'=4,'gy_0'=4,'gy_1'=2] {'gx_1'}, use_global_device_ids=true, to_apply=%add.15 | all-reduce | flops 8 | bytes 64
  225.9 6.8 %all-reduce.43 = (f32[4]{0:T(128)S(1)}, f32[4]{0:T(128)S(1)}) all-reduce(f32[4]{0:T(128)S(1)} %dynamic-update-slice.10, f32[4]{0:T(128)S(1)} %dynamic-update-slice.14), channel_id=1, replica_groups=mesh['gx_0'=4,'gx_1'=4,'gy_0'=4,'gy_1'=2] {'gy_0'}, use_global_device_ids=true, to_apply=%add.16 | all-reduce | flops 8 | bytes 64
  237.2 9.8 %all-reduce.52 = (f32[2]{0:T(128)S(1)}, f32[2]{0:T(128)S(1)}) all-reduce(f32[2]{0:T(128)S(1)} %dynamic-update-slice.11, f32[2]{0:T(128)S(1)} %dynamic-update-slice.15), channel_id=1, replica_groups=mesh['gx_0'=4,'gx_1'=4,'gy_0'=4,'gy_1'=2] {'gy_1'}, use_global_device_ids=true, to_apply=%add.17 | all-reduce | flops 4 | bytes 32
  261.5 3.7 collective-permute-start.11
  270.8 6.9 %all-to-all-start.3 = ((f32[16,1,2,32,128]{4,3,2,1,0:T(8,128)}), f32[16,1,2,32,128]{4,3,2,1,0:T(8,128)}, u32[]{:S(2)}, u32[]{:S(2)}) async-start(f32[16,1,2,32,128]{4,3,2,1,0:T(8,128)} %broadcast_in_dim.122), calls=%async_computation.3 | async-start | bytes 1048576 | tf_op jit(solution)/shard_map/all_to_all | solution.py:32
  296.5 3.8 multiply_reduce_fusion.7
  312.6 8.5 %all-reduce.48 = (f32[4]{0:T(128)S(1)}, f32[4]{0:T(128)S(1)}, f32[4]{0:T(128)S(1)}, f32[4]{0:T(128)S(1)}, f32[4]{0:T(128)S(1)}) all-reduce(f32[4]{0:T(128)S(1)} %dynamic-update-slice.16, f32[4]{0:T(128)S(1)} %dynamic-update-slice.20, f32[4]{0:T(128)S(1)} %dynamic-update-slice.32, ...), channel_id=1, replica_groups=mesh['gx_0'=4,'gx_1'=4,'gy_0'=4,'gy_1'=2] {'gx_0'}, use_global_device_ids=true, to_apply=%add.22 | all-reduce | flops 20 | bytes 160
  331.3 8.4 %all-reduce.45 = (f32[4]{0:T(128)S(1)}, f32[4]{0:T(128)S(1)}, f32[4]{0:T(128)S(1)}, f32[4]{0:T(128)S(1)}, f32[4]{0:T(128)S(1)}) all-reduce(f32[4]{0:T(128)S(1)} %dynamic-update-slice.17, f32[4]{0:T(128)S(1)} %dynamic-update-slice.21, f32[4]{0:T(128)S(1)} %dynamic-update-slice.33, ...), channel_id=1, replica_groups=mesh['gx_0'=4,'gx_1'=4,'gy_0'=4,'gy_1'=2] {'gx_1'}, use_global_device_ids=true, to_apply=%add.23 | all-reduce | flops 20 | bytes 160
  349.3 6.7 %all-reduce.42 = (f32[4]{0:T(128)S(1)}, f32[4]{0:T(128)S(1)}, f32[4]{0:T(128)S(1)}, f32[4]{0:T(128)S(1)}, f32[4]{0:T(128)S(1)}) all-reduce(f32[4]{0:T(128)S(1)} %dynamic-update-slice.18, f32[4]{0:T(128)S(1)} %dynamic-update-slice.22, f32[4]{0:T(128)S(1)} %dynamic-update-slice.34, ...), channel_id=1, replica_groups=mesh['gx_0'=4,'gx_1'=4,'gy_0'=4,'gy_1'=2] {'gy_0'}, use_global_device_ids=true, to_apply=%add.24 | all-reduce | flops 20 | bytes 160
  365.9 9.8 %all-reduce.51 = (f32[2]{0:T(128)S(1)}, f32[2]{0:T(128)S(1)}, f32[2]{0:T(128)S(1)}, f32[2]{0:T(128)S(1)}, f32[2]{0:T(128)S(1)}) all-reduce(f32[2]{0:T(128)S(1)} %dynamic-update-slice.19, f32[2]{0:T(128)S(1)} %dynamic-update-slice.23, f32[2]{0:T(128)S(1)} %dynamic-update-slice.35, ...), channel_id=1, replica_groups=mesh['gx_0'=4,'gx_1'=4,'gy_0'=4,'gy_1'=2] {'gy_1'}, use_global_device_ids=true, to_apply=%add.25 | all-reduce | flops 10 | bytes 80
  (304 shorter events, 203.3 us)
Async XLA Ops:
  0.6 18.1 %copy-start.1 = (f32[64,32,128]{2,1,0:T(8,128)S(1)}, f32[64,32,128]{2,1,0:T(8,128)}, u32[]{:S(2)}) copy-start(f32[64,32,128]{2,1,0:T(8,128)} %param.7) | copy-start | bytes 3145732
  0.7 18.1 %copy-start.9 = (f32[64,32,128]{2,1,0:T(8,128)S(1)}, f32[64,32,128]{2,1,0:T(8,128)}, u32[]{:S(2)}) copy-start(f32[64,32,128]{2,1,0:T(8,128)} %param.9) | copy-start | bytes 3145732
  1.6 22.7 %collective-permute-start = (f32[2,2,32,128]{3,2,1,0:T(8,128)S(1)}, f32[2,2,32,128]{3,2,1,0:T(8,128)S(1)}, u32[]{:S(2)}, u32[]{:S(2)}) collective-permute-start(f32[2,2,32,128]{3,2,1,0:T(8,128)S(1)} %get-tuple-element.91), channel_id=1, source_target_pairs={{0,8},{8,16},{16,24},{24,32},{32,40},{40,48},{48,56},{56,64},{64,7... | collective-permute-start | bytes 196616 | tf_op jit(solution)/shard_map/ppermute | solution.py:46
  5.6 18.8 %collective-permute-start.1 = (f32[2,2,32,128]{3,2,1,0:T(8,128)S(1)}, f32[2,2,32,128]{3,2,1,0:T(8,128)S(1)}, u32[]{:S(2)}, u32[]{:S(2)}) collective-permute-start(f32[2,2,32,128]{3,2,1,0:T(8,128)S(1)} %get-tuple-element.92), channel_id=1, source_target_pairs={{8,0},{16,8},{24,16},{32,24},{40,32},{48,40},{56,48},{64,56},{72,6... | collective-permute-start | bytes 196616 | tf_op jit(solution)/shard_map/ppermute | solution.py:47
  10.1 46.8 %all-to-all-start = ((f32[16,1,2,32,128]{4,3,2,1,0:T(8,128)}), f32[16,1,2,32,128]{4,3,2,1,0:T(8,128)}, u32[]{:S(2)}, u32[]{:S(2)}) async-start(f32[16,1,2,32,128]{4,3,2,1,0:T(8,128)} %broadcast_in_dim.119), calls=%async_computation | async-start | bytes 1048576 | tf_op jit(solution)/shard_map/all_to_all | solution.py:32
  22.1 11.1 %copy-start.32 = (u32[128]{0:T(128)S(1)}, u32[128]{0:T(128)}, u32[]{:S(2)}) copy-start(u32[128]{0:T(128)} %constant.100) | copy-start | bytes 1540
  22.1 11.7 %copy-start.31 = (u32[128]{0:T(128)S(1)}, u32[128]{0:T(128)}, u32[]{:S(2)}) copy-start(u32[128]{0:T(128)} %constant.95) | copy-start | bytes 1540
  22.1 12.3 %copy-start.30 = (f32[8]{0:T(128)S(1)}, f32[8]{0:T(128)}, u32[]{:S(2)}) copy-start(f32[8]{0:T(128)} %param.13) | copy-start | bytes 100
  24.5 10.6 %collective-permute-start.3 = (f32[2,68,2,128]{3,2,1,0:T(2,128)S(1)}, f32[2,68,2,128]{3,2,1,0:T(2,128)S(1)}, u32[]{:S(2)}, u32[]{:S(2)}) collective-permute-start(f32[2,68,2,128]{3,2,1,0:T(2,128)S(1)} %get-tuple-element.85), channel_id=1, source_target_pairs={{0,1},{1,2},{2,3},{3,4},{4,5},{5,6},{6,7},{8,9},{9,10},{10,11},{11... | collective-permute-start | bytes 417800 | tf_op jit(solution)/shard_map/ppermute | solution.py:46
  29.1 6.4 %collective-permute-start.2 = (f32[2,68,2,128]{3,2,1,0:T(2,128)S(1)}, f32[2,68,2,128]{3,2,1,0:T(2,128)S(1)}, u32[]{:S(2)}, u32[]{:S(2)}) collective-permute-start(f32[2,68,2,128]{3,2,1,0:T(2,128)S(1)} %get-tuple-element.86), channel_id=1, source_target_pairs={{1,0},{2,1},{3,2},{4,3},{5,4},{6,5},{7,6},{9,8},{10,9},{11,10},{12... | collective-permute-start | bytes 417800 | tf_op jit(solution)/shard_map/ppermute | solution.py:47
  59.0 20.9 %copy-start.4 = (f32[2,64,32,128]{3,2,1,0:T(8,128)S(1)}, f32[2,64,32,128]{3,2,1,0:T(8,128)}, u32[]{:S(2)}) copy-start(f32[2,64,32,128]{3,2,1,0:T(8,128)} %fusion.23) | copy-start | bytes 6291460
  63.7 14.9 %all-to-all-start.1 = ((f32[16,1,32,128]{3,2,1,0:T(8,128)}), f32[16,1,32,128]{3,2,1,0:T(8,128)}, u32[]{:S(2)}, u32[]{:S(2)}) async-start(f32[16,1,32,128]{3,2,1,0:T(8,128)} %broadcast_in_dim.120), calls=%async_computation.1 | async-start | bytes 524288 | tf_op jit(solution)/shard_map/all_to_all | solution.py:32
  82.5 52.1 %copy-start.28 = (pred[64,32,128]{2,1,0:T(8,128)(4,1)S(1)}, pred[64,32,128]{2,1,0:T(8,128)(4,1)}, u32[]{:S(2)}) copy-start(pred[64,32,128]{2,1,0:T(8,128)(4,1)} %get-tuple-element.93) | copy-start | bytes 786436
  149.3 6.3 %collective-permute-start.4 = (f32[2,2,32,128]{3,2,1,0:T(8,128)S(1)}, f32[2,2,32,128]{3,2,1,0:T(8,128)S(1)}, u32[]{:S(2)}, u32[]{:S(2)}) collective-permute-start(f32[2,2,32,128]{3,2,1,0:T(8,128)S(1)} %get-tuple-element.89), channel_id=1, source_target_pairs={{0,8},{8,16},{16,24},{24,32},{32,40},{40,48},{48,56},{56,64},{64,7... | collective-permute-start | bytes 196616 | tf_op jit(solution)/shard_map/ppermute | solution.py:46
  152.1 5.0 %collective-permute-start.5 = (f32[2,2,32,128]{3,2,1,0:T(8,128)S(1)}, f32[2,2,32,128]{3,2,1,0:T(8,128)S(1)}, u32[]{:S(2)}, u32[]{:S(2)}) collective-permute-start(f32[2,2,32,128]{3,2,1,0:T(8,128)S(1)} %get-tuple-element.90), channel_id=1, source_target_pairs={{8,0},{16,8},{24,16},{32,24},{40,32},{48,40},{56,48},{64,56},{72,6... | collective-permute-start | bytes 196616 | tf_op jit(solution)/shard_map/ppermute | solution.py:47
  157.2 15.2 %collective-permute-start.7 = (f32[2,68,2,128]{3,2,1,0:T(2,128)S(1)}, f32[2,68,2,128]{3,2,1,0:T(2,128)S(1)}, u32[]{:S(2)}, u32[]{:S(2)}) collective-permute-start(f32[2,68,2,128]{3,2,1,0:T(2,128)S(1)} %get-tuple-element.83), channel_id=1, source_target_pairs={{0,1},{1,2},{2,3},{3,4},{4,5},{5,6},{6,7},{8,9},{9,10},{10,11},{11... | collective-permute-start | bytes 417800 | tf_op jit(solution)/shard_map/ppermute | solution.py:46
  160.2 12.3 %collective-permute-start.6 = (f32[2,68,2,128]{3,2,1,0:T(2,128)S(1)}, f32[2,68,2,128]{3,2,1,0:T(2,128)S(1)}, u32[]{:S(2)}, u32[]{:S(2)}) collective-permute-start(f32[2,68,2,128]{3,2,1,0:T(2,128)S(1)} %get-tuple-element.84), channel_id=1, source_target_pairs={{1,0},{2,1},{3,2},{4,3},{5,4},{6,5},{7,6},{9,8},{10,9},{11,10},{12... | collective-permute-start | bytes 417800 | tf_op jit(solution)/shard_map/ppermute | solution.py:47
  165.5 21.6 %all-to-all-start.2 = ((f32[16,1,2,32,128]{4,3,2,1,0:T(8,128)}), f32[16,1,2,32,128]{4,3,2,1,0:T(8,128)}, u32[]{:S(2)}, u32[]{:S(2)}) async-start(f32[16,1,2,32,128]{4,3,2,1,0:T(8,128)} %broadcast_in_dim.121), calls=%async_computation.2 | async-start | bytes 1048576 | tf_op jit(solution)/shard_map/all_to_all | solution.py:32
  254.4 4.8 %collective-permute-start.8 = (f32[2,2,32,128]{3,2,1,0:T(8,128)S(1)}, f32[2,2,32,128]{3,2,1,0:T(8,128)S(1)}, u32[]{:S(2)}, u32[]{:S(2)}) collective-permute-start(f32[2,2,32,128]{3,2,1,0:T(8,128)S(1)} %get-tuple-element.87), channel_id=1, source_target_pairs={{0,8},{8,16},{16,24},{24,32},{32,40},{40,48},{48,56},{56,64},{64,7... | collective-permute-start | bytes 196616 | tf_op jit(solution)/shard_map/ppermute | solution.py:46
  255.7 5.0 %collective-permute-start.9 = (f32[2,2,32,128]{3,2,1,0:T(8,128)S(1)}, f32[2,2,32,128]{3,2,1,0:T(8,128)S(1)}, u32[]{:S(2)}, u32[]{:S(2)}) collective-permute-start(f32[2,2,32,128]{3,2,1,0:T(8,128)S(1)} %get-tuple-element.88), channel_id=1, source_target_pairs={{8,0},{16,8},{24,16},{32,24},{40,32},{48,40},{56,48},{64,56},{72,6... | collective-permute-start | bytes 196616 | tf_op jit(solution)/shard_map/ppermute | solution.py:47
  261.5 17.0 %collective-permute-start.11 = (f32[2,68,2,128]{3,2,1,0:T(2,128)}, f32[2,68,2,128]{3,2,1,0:T(2,128)S(1)}, u32[]{:S(2)}, u32[]{:S(2)}) collective-permute-start(f32[2,68,2,128]{3,2,1,0:T(2,128)} %get-tuple-element.81), channel_id=1, source_target_pairs={{0,1},{1,2},{2,3},{3,4},{4,5},{5,6},{6,7},{8,9},{9,10},{10,11},{11... | collective-permute-start | bytes 417800 | tf_op jit(solution)/shard_map/ppermute | solution.py:46
  265.3 13.3 %collective-permute-start.10 = (f32[2,68,2,128]{3,2,1,0:T(2,128)}, f32[2,68,2,128]{3,2,1,0:T(2,128)}, u32[]{:S(2)}, u32[]{:S(2)}) collective-permute-start(f32[2,68,2,128]{3,2,1,0:T(2,128)} %get-tuple-element.82), channel_id=1, source_target_pairs={{1,0},{2,1},{3,2},{4,3},{5,4},{6,5},{7,6},{9,8},{10,9},{11,10},{12... | collective-permute-start | bytes 417800 | tf_op jit(solution)/shard_map/ppermute | solution.py:47
  268.5 11.3 %copy-start.20 = (f32[64,32,128]{2,0,1:T(8,128)}, f32[64,32,128]{2,0,1:T(8,128)S(1)}, u32[]{:S(2)}) copy-start(f32[64,32,128]{2,0,1:T(8,128)S(1)} %get-tuple-element.135) | copy-start | bytes 3145732
  270.8 30.9 %all-to-all-start.3 = ((f32[16,1,2,32,128]{4,3,2,1,0:T(8,128)}), f32[16,1,2,32,128]{4,3,2,1,0:T(8,128)}, u32[]{:S(2)}, u32[]{:S(2)}) async-start(f32[16,1,2,32,128]{4,3,2,1,0:T(8,128)} %broadcast_in_dim.122), calls=%async_computation.3 | async-start | bytes 1048576 | tf_op jit(solution)/shard_map/all_to_all | solution.py:32
  (27 other events, 94.2 us)
